TPU v7x, 32 devices: a whole 2x2x4 slice. The times are simulated.
32 devices in a mesh: dp: 4 (over y, x), sp: 4 (over z), shift: 2 (over core).
Axes of the slice: x: 2, y: 2, z: 4, core: 2. Of those that a mesh axis runs over, the one named last changes fastest.
Arguments:
- query_rows: bfloat16 [8, 1024, 32, 128], P(('shift', 'dp'), 'sp'), parts along dimension 0, may hold values from -6 to 6
- key_rows: bfloat16 [8, 1024, 32, 128], P(('shift', 'dp'), 'sp'), parts along dimension 0, may hold values from -6 to 6
- value_rows: bfloat16 [8, 1024, 32, 128], P(('shift', 'dp'), 'sp'), parts along dimension 0, may hold values from -6 to 6
- out_weight: bfloat16 [8192, 4096], P(('shift', 'dp')), parts along dimension 0, may hold values from -0.09375 to 0.09375
Outputs:
- mixer_out: bfloat16 [8, 1024, 4096], P(('shift', 'dp'), 'sp'), parts along dimension 0
There are 2 independent parts, one for each index of `shift`. A program takes and returns all parts, laid end to end along the dimension named above; each array names one. Nothing has to cross between parts.
All inputs are finite; a program needn't handle non-finite values.
Results may differ from a plain program's by a relative error of at most 0.006.
Values may be sent and summed in bfloat16 or wider, within the bound.
A program may use at most 128 MiB of HBM per device.

v0:
```python
import functools

import jax
import jax.numpy as jnp
from jax import lax
from jax.experimental import pallas as pl
from jax.experimental.pallas import tpu as pltpu
from jax.sharding import PartitionSpec as P


def feature_map(values):
    wide = values.astype(jnp.float32)
    return jnp.where(wide > 0.0, wide + 1.0, jnp.exp(jnp.minimum(wide, 0.0))).astype(jnp.bfloat16)


def plain_body(query_rows, key_rows, value_rows, out_weight):
    query_feature, key_feature = (feature_map(query_rows), feature_map(key_rows))
    count = query_rows.shape[1] * lax.axis_size("sp")
    state = (
        jnp.einsum("bthd,bthe->bhde", key_feature, value_rows, preferred_element_type=jnp.float32)
        / count
    )
    mass = jnp.sum(key_feature.astype(jnp.float32), axis=1) / count
    state = lax.psum(state.astype(jnp.bfloat16), "sp")
    mass = lax.psum(mass, "sp")
    top = jnp.einsum("bthd,bhde->bthe", query_feature, state, preferred_element_type=jnp.float32)
    bottom = jnp.einsum(
        "bthd,bhd->bth", query_feature.astype(jnp.float32), mass, precision=lax.Precision.HIGHEST
    )
    mixed = (top / (bottom + 0.001)[..., None] * count**0.5).astype(jnp.bfloat16)
    mixed = mixed.reshape(mixed.shape[0], mixed.shape[1], -1)
    mine = lax.all_to_all(mixed, "dp", split_axis=2, concat_axis=0, tiled=True)
    part = jnp.einsum("btw,wv->btv", mine, out_weight, preferred_element_type=jnp.float32)
    return lax.psum_scatter(part.astype(jnp.bfloat16), "dp", scatter_dimension=0, tiled=True)


MESH = pl.DeviceIdType.MESH
EXTRA = 16
NT = (((1,), (1,)), ((), ()))


def remote(src, dst, send, recv, **where):
    return pltpu.make_async_remote_copy(
        src_ref=src, dst_ref=dst, send_sem=send, recv_sem=recv, device_id=where, device_id_type=MESH
    )


def kernel(
    ND, NS, A, B, count, q_hbm, st_ref, w_hbm, out_ref,
    qraw, qwide, q_ref, w, qall, st1, red, stall, mixed, part, r1e, r1o, s2e, s2o, keep, r2e, r2o,
    wsem, qsem, lsem, qs, qr, ss1, rs1, ss2, rs2, e1s, e1r, o1s, o1r, e2s, e2r, o2s, o2r,
):
    d, p = lax.axis_index("dp"), lax.axis_index("sp")
    i, j = lax.div(d, B), lax.rem(d, B)
    HD, HS, size = q_ref.shape[1], st_ref.shape[2], q_ref.shape[3]
    half, C = part.shape[0] // 2, part.shape[-1]

    def at(base, r, n):
        return lax.rem(base + r + n, n)

    def twin(r):
        other, bit = p, 1
        while bit <= r:
            if r & bit:
                other = other + bit - 2 * bit * lax.rem(lax.div(p, bit), 2)
            bit *= 2
        return other

    load = pltpu.make_async_copy(q_hbm, qraw, qsem)
    load.start()
    weights = pltpu.make_async_copy(w_hbm, w, wsem)
    weights.start()

    barrier = pltpu.get_barrier_semaphore()
    for rd in range(ND):
        for rp in range(NS):
            if rd or rp:
                pl.semaphore_signal(
                    barrier, inc=1, device_id={"dp": at(d, rd, ND), "sp": at(p, rp, NS)}, device_id_type=MESH
                )
    pl.semaphore_wait(barrier, ND * NS - 1)

    order = list(range(NS - 1, 0, -1))
    first = {}
    for rd in range(ND):
        dd = at(d, rd, ND)
        for r in order:
            pp = twin(r)
            first[rd, r] = remote(
                st_ref.at[dd, pp], st1.at[r - 1, dd], ss1.at[rd, r], rs1.at[rd, r], sp=pp
            )
            first[rd, r].start()

    load.wait()
    tokens, heads, step = q_ref.shape[2], ND * HD, 1024

    @pl.loop(0, tokens * heads // step)
    def _(x):
        rows = pl.ds(pl.multiple_of(x * step, step), step)
        wide = qraw[rows].astype(jnp.float32)
        qwide[rows] = jnp.where(wide > 0.0, wide + 1.0, jnp.exp(jnp.minimum(wide, 0.0)))

    @pl.loop(0, ND)
    def _(x):
        for k in range(HD):
            q_ref[x, k] = qwide[pl.ds(x * HD + k, tokens, stride=heads), :].astype(q_ref.dtype)

    queries = {}
    for r in range(1, ND):
        dd = at(d, r, ND)
        queries[r] = remote(q_ref.at[dd], qall.at[d], qs.at[r], qr.at[r], dp=dd)
        queries[r].start()
    own_query = pltpu.make_async_copy(q_ref.at[d], qall.at[d], lsem.at[0])
    own_query.start()

    second = {}
    for rd in range(ND):
        dd = at(d, rd, ND)
        total = st_ref[dd, p].astype(jnp.float32)
        for r in order:
            first[rd, r].wait_recv()
            total += st1[r - 1, dd].astype(jnp.float32)
        red[dd] = total.astype(red.dtype)
        for rp in [0] + order:
            if rd or rp:
                second[rd, rp] = remote(
                    red.at[dd], stall.at[d, p], ss2.at[rd, rp], rs2.at[rd, rp], dp=dd, sp=twin(rp)
                )
                second[rd, rp].start()
            else:
                own_state = pltpu.make_async_copy(red.at[d], stall.at[d, p], lsem.at[1])
                own_state.start()

    for rp in [0] + order:
        pp = twin(rp)
        for rd in range(ND):
            s = at(d, -rd, ND)
            if rp == 0 and rd:
                remote(q_ref.at[d], qall.at[s], qs.at[rd], qr.at[rd], dp=s).wait_recv()
            if rd or rp:
                remote(red.at[d], stall.at[s, pp], ss2.at[rd, rp], rs2.at[rd, rp], dp=s, sp=pp).wait_recv()
            else:
                own_query.wait()
                own_state.wait()

        @pl.loop(0, ND)
        def _(s):
            for k in range(HS):
                head = pp * HS + k
                both = stall[s, pp, k]
                both = jnp.concatenate([both[:size]] + [both[size:]] * (size // EXTRA), axis=0)
                read = lax.dot_general(qall[s, head], both, NT, preferred_element_type=jnp.float32)
                read = read[:, :size] / (read[:, size:] + 0.001) * count**0.5
                mixed[s, :, pl.ds(pl.multiple_of(head * size, size), size)] = read.astype(mixed.dtype)

    weights.wait()

    def e1(c, r):
        jj = at(j, r, B)
        return remote(part.at[2 * c, :, jj], r1e.at[c, r - 1], e1s.at[c, r], e1r.at[c, r], dp=i * B + jj)

    def o1(c, r):
        ii = at(i, r, A)
        return remote(part.at[2 * c + 1, ii], r1o.at[c, r - 1], o1s.at[c, r], o1r.at[c, r], dp=ii * B + j)

    def e2(c, r):
        ii = at(i, r, A)
        return remote(s2e.at[c, ii], r2e.at[c, r - 1], e2s.at[c, r], e2r.at[c, r], dp=ii * B + j)

    def o2(c, r):
        jj = at(j, r, B)
        return remote(s2o.at[c, jj], r2o.at[c, r - 1], o2s.at[c, r], o2r.at[c, r], dp=i * B + jj)

    @pl.loop(0, half)
    def _(c):
        for odd in range(2):
            columns = pl.ds(pl.multiple_of((2 * c + odd) * C, C), C)

            @pl.loop(0, ND)
            def _(s):
                block = jnp.dot(mixed[s], w[:, columns], preferred_element_type=jnp.float32)
                part[2 * c + odd, lax.div(s, B), lax.rem(s, B)] = block.astype(part.dtype)

            for r in range(1, A if odd else B):
                (o1 if odd else e1)(c, r).start()

    @pl.loop(0, half)
    def _(c):
        for r in range(1, B):
            e1(c, r).wait_recv()
        for r in range(A):
            ii = at(i, r, A)
            total = part[2 * c, ii, j].astype(jnp.float32)
            for k in range(1, B):
                total += r1e[c, k - 1, ii].astype(jnp.float32)
            if r:
                s2e[c, ii] = total.astype(s2e.dtype)
                e2(c, r).start()
            else:
                keep[2 * c] = total
        for r in range(1, A):
            o1(c, r).wait_recv()
        for r in range(B):
            jj = at(j, r, B)
            total = part[2 * c + 1, i, jj].astype(jnp.float32)
            for k in range(1, A):
                total += r1o[c, k - 1, jj].astype(jnp.float32)
            if r:
                s2o[c, jj] = total.astype(s2o.dtype)
                o2(c, r).start()
            else:
                keep[2 * c + 1] = total

    @pl.loop(0, half)
    def _(c):
        for odd, n, copies, slots in ((0, A, e2, r2e), (1, B, o2, r2o)):
            total = keep[2 * c + odd]
            for r in range(1, n):
                copies(c, r).wait_recv()
                total += slots[c, r - 1].astype(jnp.float32)
            columns = pl.ds(pl.multiple_of((2 * c + odd) * C, C), C)
            out_ref[:, columns] = total.astype(out_ref.dtype)

    for r in range(1, ND):
        queries[r].wait_send()
    for copy in list(first.values()) + list(second.values()):
        copy.wait_send()

    @pl.loop(0, half)
    def _(c):
        for r in range(1, B):
            e1(c, r).wait_send()
            o2(c, r).wait_send()
        for r in range(1, A):
            o1(c, r).wait_send()
            e2(c, r).wait_send()


def split_of(n):
    for a in range(int(n**0.5), 0, -1):
        if n % a == 0:
            return a, n // a


def kernel_body(query_rows, key_rows, value_rows, out_weight):
    ND, NS = lax.axis_size("dp"), lax.axis_size("sp")
    _, T, H, size = query_rows.shape
    V, rows = out_weight.shape[1], out_weight.shape[0]
    A, B = split_of(ND)
    HD, HS, NC = H // ND, H // ND // NS, 16
    C, half, count = V // NC, NC // 2, T * NS
    key_feature = feature_map(key_rows)
    state = jnp.einsum(
        "bthd,bthe->bhed", key_feature, value_rows, preferred_element_type=jnp.float32
    )[0] / count
    mass = jnp.sum(key_feature.astype(jnp.float32), axis=1)[0] / count
    mass = jnp.broadcast_to(mass[:, None, :].astype(jnp.bfloat16), (H, EXTRA, size))
    state = jnp.concatenate([state.astype(jnp.bfloat16), mass], axis=1).reshape(ND, NS, HS, size + EXTRA, size)
    query = query_rows.reshape(T * H, size)
    bf, block = jnp.bfloat16, (HS, size + EXTRA, size)
    dma = pltpu.SemaphoreType.DMA
    out = pl.pallas_call(
        functools.partial(kernel, ND, NS, A, B, count),
        out_shape=jax.ShapeDtypeStruct((T, V), bf),
        in_specs=[
            pl.BlockSpec(memory_space=pl.ANY),
            pl.BlockSpec(memory_space=pltpu.VMEM),
            pl.BlockSpec(memory_space=pl.ANY),
        ],
        out_specs=pl.BlockSpec(memory_space=pltpu.VMEM),
        scratch_shapes=[
            pltpu.VMEM((T * H, size), bf),
            pltpu.VMEM((T * H, size), jnp.float32),
            pltpu.VMEM((ND, HD, T, size), bf),
            pltpu.VMEM((rows, V), bf),
            pltpu.VMEM((ND, HD, T, size), bf),
            pltpu.VMEM((NS - 1, ND) + block, bf),
            pltpu.VMEM((ND,) + block, bf),
            pltpu.VMEM((ND, NS) + block, bf),
            pltpu.VMEM((ND, T, HD * size), bf),
            pltpu.VMEM((NC, A, B, T, C), bf),
            pltpu.VMEM((half, B - 1, A, T, C), bf),
            pltpu.VMEM((half, A - 1, B, T, C), bf),
            pltpu.VMEM((half, A, T, C), bf),
            pltpu.VMEM((half, B, T, C), bf),
            pltpu.VMEM((NC, T, C), jnp.float32),
            pltpu.VMEM((half, A - 1, T, C), bf),
            pltpu.VMEM((half, B - 1, T, C), bf),
            dma, dma, dma((2,)), dma((ND,)), dma((ND,)), dma((ND, NS)), dma((ND, NS)), dma((ND, NS)), dma((ND, NS)),
            dma((half, B)), dma((half, B)), dma((half, A)), dma((half, A)),
            dma((half, A)), dma((half, A)), dma((half, B)), dma((half, B)),
        ],
        compiler_params=pltpu.CompilerParams(
            collective_id=0, has_side_effects=True, vmem_limit_bytes=63 * 2**20
        ),
    )(query, state, out_weight)
    return out[None]


def body(query_rows, key_rows, value_rows, out_weight):
    ND, NS = lax.axis_size("dp"), lax.axis_size("sp")
    batch, T, H, size = query_rows.shape
    rows, V = out_weight.shape
    need = 2 * rows * V + 2 * ND * T * V * 2 + 2 * T * V * 8 + 6 * H * T * size * 2
    fits = batch == 1 and H % (ND * NS) == 0 and V % 2048 == 0 and min(split_of(ND)) > 1
    fits = fits and size == 128 and T % 16 == 0 and T * H % 1024 == 0 and NS & (NS - 1) == 0 and need < 56 * 2**20
    run = kernel_body if fits else plain_body
    return run(query_rows, key_rows, value_rows, out_weight)


def solution(mesh):
    placed = (
        P(("shift", "dp"), "sp", None, None),
        P(("shift", "dp"), "sp", None, None),
        P(("shift", "dp"), "sp", None, None),
        P(("shift", "dp"), None),
    )
    return jax.shard_map(
        body, mesh=mesh, in_specs=placed, out_specs=P(("shift", "dp"), "sp", None), check_vma=False
    )
```

profile of v0, /device:TPU:0, one launch (start us, length us, event | category | flops | bytes accessed | tf_op | source)
XLA Modules:
  0.0 145.8 jit_solution(9967343616057212787)
XLA Ops:
  0.0 0.0 copy-start
  0.0 3.0 %fusion.10 = (bf16[256,32,128]{2,1,0:T(8,128)(2,1)S(1)}, f32[32,128]{1,0:T(8,128)S(1)}) fusion(bf16[1,256,32,128]{3,2,1,0:T(8,128)(2,1)} %param.5), kind=kLoop, calls=%fused_computation.12 | loop fusion | flops 8384512 | bytes 4210688 | tf_op jit(solution)/shard_map/reshape.1
  3.0 0.0 copy-done
  3.0 1.6 %multiply_convert_fusion = bf16[32,128,128]{1,2,0:T(8,128)(2,1)S(1)} fusion(bf16[256,32,128]{2,1,0:T(8,128)(2,1)S(1)} %get-tuple-element.5, bf16[256,32,128]{2,1,0:T(8,128)(2,1)S(1)} %bitcast.13), kind=kOutput, calls=%fused_computation.10 | convolution fusion | flops 269484032 | bytes 5242880 | tf_op jit(solution)/shard_map/bthd,bthe->bhed/dot_general | solution.py:253
  4.6 1.1 pad_maximum_fusion.st_ref
  5.7 136.9 %shard_map.46 = bf16[256,4096]{1,0:T(8,128)(2,1)} custom-call(bf16[8192,128]{1,0:T(8,128)(2,1)} %bitcast.10, bf16[4,4,2,144,128]{4,3,2,1,0:T(8,128)(2,1)} %pad_maximum_fusion.st_ref, bf16[1024,4096]{1,0:T(8,128)(2,1)} %w_hbm.1), custom_call_target="tpu_custom_call" | custom-call | tf_op jit(solution)/shard_map/pallas_call | solution.py:262
  142.6 3.1 %copy.16 = bf16[1,256,4096]{2,1,0:T(8,128)(2,1)} copy(bf16[1,256,4096]{2,1,0:T(8,128)(2,1)} %bitcast.9) | data formatting | bytes 4194304
  (2 shorter events, 0.0 us)
Async XLA Ops:
  0.0 3.0 %copy-start = (bf16[1,256,32,128]{3,2,1,0:T(8,128)(2,1)S(1)}, bf16[1,256,32,128]{3,2,1,0:T(8,128)(2,1)}, u32[]{:S(2)}) copy-start(bf16[1,256,32,128]{3,2,1,0:T(8,128)(2,1)} %param.6) | copy-start | bytes 6291460
where the time goes:
time: 146 us
  Pallas kernels  137 us (94%)
  other arithmetic  4.07 us (3%)
  local copies, waits for them, and re-layouts  3.15 us (2%)
  matrix products  1.57 us (1%)
    pallas_call x1, Pallas kernels, kernel_body(): pl.pallas_call(functools.partial(kernel, ND, NS, A, B, count), out_shape=...  137 us
    unnamed x3, local copies, waits for them, and re-layouts  3.13 us
    another operation x1, other arithmetic  2.96 us

commit v1 on v0

v1 whole, which is shorter than its diff:
```python
import functools

import jax
import jax.numpy as jnp
from jax import lax
from jax.experimental import pallas as pl
from jax.experimental.pallas import tpu as pltpu
from jax.sharding import PartitionSpec as P


def feature_map(values):
    wide = values.astype(jnp.float32)
    return jnp.where(wide > 0.0, wide + 1.0, jnp.exp(jnp.minimum(wide, 0.0))).astype(jnp.bfloat16)


def plain_body(query_rows, key_rows, value_rows, out_weight):
    query_feature, key_feature = (feature_map(query_rows), feature_map(key_rows))
    count = query_rows.shape[1] * lax.axis_size("sp")
    state = (
        jnp.einsum("bthd,bthe->bhde", key_feature, value_rows, preferred_element_type=jnp.float32)
        / count
    )
    mass = jnp.sum(key_feature.astype(jnp.float32), axis=1) / count
    state = lax.psum(state.astype(jnp.bfloat16), "sp")
    mass = lax.psum(mass, "sp")
    top = jnp.einsum("bthd,bhde->bthe", query_feature, state, preferred_element_type=jnp.float32)
    bottom = jnp.einsum(
        "bthd,bhd->bth", query_feature.astype(jnp.float32), mass, precision=lax.Precision.HIGHEST
    )
    mixed = (top / (bottom + 0.001)[..., None] * count**0.5).astype(jnp.bfloat16)
    mixed = mixed.reshape(mixed.shape[0], mixed.shape[1], -1)
    mine = lax.all_to_all(mixed, "dp", split_axis=2, concat_axis=0, tiled=True)
    part = jnp.einsum("btw,wv->btv", mine, out_weight, preferred_element_type=jnp.float32)
    return lax.psum_scatter(part.astype(jnp.bfloat16), "dp", scatter_dimension=0, tiled=True)


MESH = pl.DeviceIdType.MESH
NT = (((1,), (1,)), ((), ()))
TN = (((0,), (0,)), ((), ()))
EXTRA = 16
PART = 4


def feature32(values):
    wide = values.astype(jnp.float32)
    return jnp.where(wide > 0.0, wide + 1.0, jnp.exp(jnp.minimum(wide, 0.0)))


def remote(src, dst, send, recv, **where):
    return pltpu.make_async_remote_copy(
        src_ref=src, dst_ref=dst, send_sem=send, recv_sem=recv, device_id=where, device_id_type=MESH
    )


def kernel(
    NS, count, q_hbm, k_hbm, v_hbm, w_hbm, out_hbm,
    kin, vin, qin, wide, wide2, w, own, up, inb, cb, sall, qf, mixed,
    m1, r1, s2, r2, keep, outv,
    ksem, vsem, lsem, wsem, osem, qs, qr, us, inr, cbr, ds, sts, str_, s1, t1, s2s, s2r,
):
    d, p = lax.axis_index("dp"), lax.axis_index("sp")
    i, j = lax.div(d, 2), lax.rem(d, 2)
    T, HD, size = kin.shape[1:]
    G, SUB = up.shape[0], sall.shape[1]
    NC, C = keep.shape[0], keep.shape[2]
    half, mid = NC // 2, NS // 2

    def peer(r):
        return lax.rem(i + r // 2, 2) * 2 + lax.rem(j + r % 2, 2)

    left = p < mid
    side = 1 - lax.div(p, mid)
    center = p - 1 + 2 * side
    outer = p + 1 - 2 * side
    is_mid = jnp.logical_or(p == mid - 1, p == mid)
    has_outer = jnp.logical_and(p > 0, p < NS - 1)
    has_inner = jnp.logical_not(is_mid)

    loads = {}
    for n in range(4):
        rows = pl.ds(peer((n + 1) % 4) * HD, HD)
        loads[n] = (
            pltpu.make_async_copy(k_hbm.at[:, rows], kin.at[n], ksem.at[n]),
            pltpu.make_async_copy(v_hbm.at[:, rows], vin.at[n], vsem.at[n]),
        )
        loads[n][0].start()
        loads[n][1].start()

    barrier = pltpu.get_barrier_semaphore()
    for r in (1, 2, 3):
        pl.semaphore_signal(barrier, inc=1, device_id={"dp": peer(r)}, device_id_type=MESH)
    pl.semaphore_signal(barrier, inc=1, device_id={"sp": center}, device_id_type=MESH)

    @pl.when(has_outer)
    def _():
        pl.semaphore_signal(barrier, inc=1, device_id={"sp": outer}, device_id_type=MESH)
        pl.semaphore_wait(barrier, 5)

    @pl.when(jnp.logical_not(has_outer))
    def _():
        pl.semaphore_wait(barrier, 4)

    queries = {}
    for r in (1, 2, 3):
        rows = pl.ds(peer(r) * HD, HD)
        queries[r] = remote(q_hbm.at[:, rows], qin.at[r], qs.at[r], qr.at[r], dp=peer(r))
        queries[r].start()
    own_query = pltpu.make_async_copy(q_hbm.at[:, pl.ds(d * HD, HD)], qin.at[0], lsem)
    own_query.start()
    weights = pltpu.make_async_copy(w_hbm, w, wsem)
    weights.start()

    def widen(src, dst, fn):
        step = 64

        @pl.loop(0, T // step)
        def _(x):
            block = fn(src[pl.ds(pl.multiple_of(x * step, step), step)])
            rows = step * HD
            dst[pl.ds(pl.multiple_of(x * rows, rows), rows)] = block.reshape(rows, size)

    def up_end(g):
        return remote(up.at[g], inb.at[g], us.at[g], inr.at[g], sp=center)

    def up_mid(g):
        return remote(up.at[g], cb.at[g], us.at[g], cbr.at[g], sp=center)

    def down(g):
        return remote(cb.at[g], cb.at[g], ds.at[g], cbr.at[g], sp=outer)

    def spread(g):
        n, x = lax.div(g, SUB), lax.rem(g, SUB)
        r = lax.rem(n + 1, 4)
        dd = lax.rem(i + lax.div(r, 2), 2) * 2 + lax.rem(j + lax.rem(r, 2), 2)
        return remote(cb.at[g], sall.at[n, x], sts.at[g], str_.at[n, x], dp=dd)

    for n in range(4):
        loads[n][0].wait()
        loads[n][1].wait()
        widen(kin.at[n], wide, feature32)
        widen(vin.at[n], wide2, lambda x: x.astype(jnp.float32))

        @pl.loop(0, SUB)
        def _(x):
            g = n * SUB + x
            row = lax.broadcasted_iota(jnp.int32, (EXTRA, size), 0)
            masses = jnp.zeros((EXTRA, size), jnp.float32)
            for k in range(PART):
                key = wide[pl.ds(x * PART + k, T, stride=HD), :].astype(jnp.bfloat16)
                value = wide2[pl.ds(x * PART + k, T, stride=HD), :].astype(jnp.bfloat16)
                state = lax.dot_general(value, key, TN, preferred_element_type=jnp.float32) / count
                mass = jnp.sum(key.astype(jnp.float32), axis=0, keepdims=True) / count
                masses = jnp.where(row == k, mass, masses)
                own[g, k * size : (k + 1) * size] = state
                up[g, k * size : (k + 1) * size] = state.astype(up.dtype)
            own[g, PART * size :] = masses
            up[g, PART * size :] = masses.astype(up.dtype)

            @pl.when(has_inner)
            def _():
                up_end(g).start()

    def take_in(g):
        up_end(g).wait_recv()
        total = own[g] + inb[g].astype(jnp.float32)
        own[g] = total
        up[g] = total.astype(up.dtype)
        up_mid(g).start()

    def finish(g):
        up_mid(g).wait_recv()

        @pl.when(is_mid)
        def _():
            cb[g] = (own[g] + cb[g].astype(jnp.float32)).astype(cb.dtype)

        @pl.when(has_outer)
        def _():
            down(g).start()

    LAG = min(2, SUB)

    def reduce_states(first, last, send):
        @pl.when(is_mid)
        def _():
            for g in range(first, min(first + LAG, last)):
                take_in(g)

        @pl.loop(first, last)
        def _(g):
            @pl.when(jnp.logical_and(is_mid, g + LAG < last))
            def _():
                take_in(g + LAG)

            finish(g)
            if send:
                spread(g).start()

    def query_features(r):
        widen(qin.at[r], wide, feature32)
        for k in range(HD):
            qf[r, k] = wide[pl.ds(k, T, stride=HD), :].astype(qf.dtype)

    def mix(r, states):
        for k in range(HD):
            x, kk = k // PART, k % PART
            block = states(x)
            masses = block[PART * size :].astype(jnp.float32)
            mass = jnp.broadcast_to(masses[kk : kk + 1], (size, size)).astype(jnp.bfloat16)
            both = jnp.concatenate([block[kk * size : (kk + 1) * size], mass], axis=0)
            read = lax.dot_general(qf[r, k], both, NT, preferred_element_type=jnp.float32)
            read = read[:, :size] / (read[:, size:] + 0.001) * count**0.5
            mixed[r, :, k * size : (k + 1) * size] = read.astype(mixed.dtype)

    def wait_spread(n):
        for x in range(SUB):
            remote(cb.at[0], sall.at[n, x], sts.at[0], str_.at[n, x], dp=d).wait_recv()

    def columns(c, odd):
        return pl.ds(pl.multiple_of((2 * c + odd) * C, C), C)

    def first(c, odd, diagonal):
        return remote(
            m1.at[odd, c, diagonal], r1.at[odd, c, diagonal], s1.at[odd, c, diagonal], t1.at[odd, c, diagonal],
            dp=peer(2 if odd else 1),
        )

    def second(c, odd):
        return remote(s2.at[odd, c], r2.at[odd, c], s2s.at[odd, c], s2r.at[odd, c], dp=peer(1 if odd else 2))

    def times(r, c, odd):
        return jnp.dot(mixed[r], w[:, columns(c, odd)], preferred_element_type=jnp.float32)

    reduce_states(0, 3 * SUB, True)
    for r in (1, 2):
        queries[r].wait_recv()
        query_features(r)
    for r in (1, 2):
        wait_spread(r - 1)
        mix(r, lambda x: sall[r - 1, x])
    weights.wait()

    @pl.loop(0, half)
    def _(c):
        for odd in range(2):
            m1[odd, c, 0] = times(2 if odd else 1, c, odd).astype(m1.dtype)
            first(c, odd, 0).start()

    queries[3].wait_recv()
    query_features(3)
    reduce_states(3 * SUB, 4 * SUB, False)
    wait_spread(2)
    mix(3, lambda x: sall[2, x])

    @pl.loop(0, half)
    def _(c):
        for odd in range(2):
            m1[odd, c, 1] = times(3, c, odd).astype(m1.dtype)
            first(c, odd, 1).start()

    own_query.wait()
    query_features(0)
    mix(0, lambda x: cb[3 * SUB + x])

    @pl.loop(0, half)
    def _(c):
        for odd in range(2):
            block = times(0, c, odd)
            first(c, odd, 0).wait_recv()
            keep[2 * c + odd] = block + r1[odd, c, 0].astype(jnp.float32)

    @pl.loop(0, half)
    def _(c):
        for odd in range(2):
            block = times(1 if odd else 2, c, odd)
            first(c, odd, 1).wait_recv()
            s2[odd, c] = (block + r1[odd, c, 1].astype(jnp.float32)).astype(s2.dtype)
            second(c, odd).start()

    def leave(c, odd):
        return pltpu.make_async_copy(outv.at[2 * c + odd], out_hbm.at[:, columns(c, odd)], osem.at[2 * c + odd])

    @pl.loop(0, half)
    def _(c):
        for odd in range(2):
            second(c, odd).wait_recv()
            outv[2 * c + odd] = (keep[2 * c + odd] + r2[odd, c].astype(jnp.float32)).astype(outv.dtype)
            leave(c, odd).start()

    for r in (1, 2, 3):
        queries[r].wait_send()

    @pl.loop(0, G)
    def _(g):
        up_end(g).wait_send()

        @pl.when(has_outer)
        def _():
            down(g).wait_send()

    @pl.loop(0, 3 * SUB)
    def _(g):
        spread(g).wait_send()

    @pl.loop(0, half)
    def _(c):
        for odd in range(2):
            first(c, odd, 0).wait_send()
            first(c, odd, 1).wait_send()
            second(c, odd).wait_send()
            leave(c, odd).wait()


def kernel_body(query_rows, key_rows, value_rows, out_weight):
    NS = lax.axis_size("sp")
    _, T, H, size = query_rows.shape
    V, rows = out_weight.shape[1], out_weight.shape[0]
    HD, NC = H // 4, 16
    C, half, count = V // NC, NC // 2, T * NS
    SUB = HD // PART
    G, R = 4 * SUB, PART * size + EXTRA
    bf, f32 = jnp.bfloat16, jnp.float32
    dma = pltpu.SemaphoreType.DMA
    hbm = pl.BlockSpec(memory_space=pl.ANY)
    out = pl.pallas_call(
        functools.partial(kernel, NS, count),
        out_shape=jax.ShapeDtypeStruct((T, V), bf),
        in_specs=[hbm] * 4,
        out_specs=hbm,
        scratch_shapes=[
            pltpu.VMEM((4, T, HD, size), bf),
            pltpu.VMEM((4, T, HD, size), bf),
            pltpu.VMEM((4, T, HD, size), bf),
            pltpu.VMEM((T * HD, size), f32),
            pltpu.VMEM((T * HD, size), f32),
            pltpu.VMEM((rows, V), bf),
            pltpu.VMEM((G, R, size), f32),
            pltpu.VMEM((G, R, size), bf),
            pltpu.VMEM((G, R, size), bf),
            pltpu.VMEM((G, R, size), bf),
            pltpu.VMEM((3, SUB, R, size), bf),
            pltpu.VMEM((4, HD, T, size), bf),
            pltpu.VMEM((4, T, rows), bf),
            pltpu.VMEM((2, half, 2, T, C), bf),
            pltpu.VMEM((2, half, 2, T, C), bf),
            pltpu.VMEM((2, half, T, C), bf),
            pltpu.VMEM((2, half, T, C), bf),
            pltpu.VMEM((NC, T, C), f32),
            pltpu.VMEM((NC, T, C), bf),
            dma((4,)), dma((4,)), dma, dma, dma((NC,)), dma((4,)), dma((4,)),
            dma((G,)), dma((G,)), dma((G,)), dma((G,)), dma((3 * SUB,)), dma((3, SUB)),
            dma((2, half, 2)), dma((2, half, 2)), dma((2, half)), dma((2, half)),
        ],
        compiler_params=pltpu.CompilerParams(
            collective_id=0, has_side_effects=True, vmem_limit_bytes=60 * 2**20
        ),
    )(query_rows[0], key_rows[0], value_rows[0], out_weight)
    return out[None]


def split_of(n):
    for a in range(int(n**0.5), 0, -1):
        if n % a == 0:
            return a, n // a


def body(query_rows, key_rows, value_rows, out_weight):
    ND, NS = lax.axis_size("dp"), lax.axis_size("sp")
    batch, T, H, size = query_rows.shape
    rows, V = out_weight.shape
    fits = batch == 1 and split_of(ND) == (2, 2) and NS == 4 and H % 4 == 0 and (H // 4) % 8 == 0
    fits = fits and size == 128 and T % 64 == 0 and V % 4096 == 0 and rows * 4 == H * size
    need = 2 * rows * V + 18 * T * V + 12 * T * H * size + 14 * H * size * size
    run = kernel_body if fits and need < 50 * 2**20 else plain_body
    return run(query_rows, key_rows, value_rows, out_weight)


def solution(mesh):
    placed = (
        P(("shift", "dp"), "sp", None, None),
        P(("shift", "dp"), "sp", None, None),
        P(("shift", "dp"), "sp", None, None),
        P(("shift", "dp"), None),
    )
    return jax.shard_map(
        body, mesh=mesh, in_specs=placed, out_specs=P(("shift", "dp"), "sp", None), check_vma=False
    )
```

time: 146 us -> 113 us (0.77)
  Pallas kernels: 137 us -> 110 us
  other arithmetic: 4.07 us -> 0 us
  matrix products: 1.57 us -> 0 us
    pallas_call x1, Pallas kernels: 137 us -> 110 us  [kernel_body(): pl.pallas_call(functools.partial(kernel, NS, count), out_shape=jax.ShapeD...]
    another operation x1 -> x0, other arithmetic: 2.96 us -> none
    dot_general x1 -> x0, matrix products: 1.57 us -> none  [kernel_body(): jnp.einsum('bthd,bthe->bhed', key_feature, value_rows, preferred_element_...]
    unnamed x3 -> x1, local copies, waits for them, and re-layouts: 3.13 us -> 3.13 us
where the time goes in v1:
time: 113 us
  Pallas kernels  110 us (97%)
  local copies, waits for them, and re-layouts  3.13 us (3%)
    pallas_call x1, Pallas kernels, kernel_body(): pl.pallas_call(functools.partial(kernel, NS, count), out_shape=jax.ShapeD...  110 us
    unnamed x1, local copies, waits for them, and re-layouts  3.13 us

profile of v1, /device:TPU:0, one launch (start us, length us, event | category | flops | bytes accessed | tf_op | source)
XLA Modules:
  0.0 113.1 jit_solution(11099677908649031300)
XLA Ops:
  0.0 110.0 %shard_map.46 = bf16[256,4096]{1,0:T(8,128)(2,1)} custom-call(bf16[256,32,128]{2,1,0:T(8,128)(2,1)} %bitcast.5, bf16[256,32,128]{2,1,0:T(8,128)(2,1)} %bitcast.6, bf16[256,32,128]{2,1,0:T(8,128)(2,1)} %bitcast.7, bf16[1024,4096]{1,0:T(8,128)(2,1)} %w_hbm.1), custom_call_target="tpu_custom_call" | custom-call | tf_op jit(solution)/shard_map/pallas_call | solution.py:325
  110.0 3.1 %copy.6 = bf16[1,256,4096]{2,1,0:T(8,128)(2,1)} copy(bf16[1,256,4096]{2,1,0:T(8,128)(2,1)} %bitcast.4) | data formatting | bytes 4194304

commit v2 on v1

--- a/solution.py
+++ b/solution.py
@@ -38,7 +38,7 @@
 NT = (((1,), (1,)), ((), ()))
 TN = (((0,), (0,)), ((), ()))
 EXTRA = 16
-PART = 4
+PART = 2
 
 
 def feature32(values):
@@ -55,15 +55,17 @@
 def kernel(
     NS, count, q_hbm, k_hbm, v_hbm, w_hbm, out_hbm,
     kin, vin, qin, wide, wide2, w, own, up, inb, cb, sall, qf, mixed,
-    m1, r1, s2, r2, keep, outv,
-    ksem, vsem, lsem, wsem, osem, qs, qr, us, inr, cbr, ds, sts, str_, s1, t1, s2s, s2r,
+    m1, r1, s2, r2, keep,
+    ksem, vsem, lsem, wsem, qs, qr, us, inr, cbr, ds, sts, fws, str_, s1, t1, s2s, s2r,
 ):
     d, p = lax.axis_index("dp"), lax.axis_index("sp")
     i, j = lax.div(d, 2), lax.rem(d, 2)
     T, HD, size = kin.shape[1:]
     G, SUB = up.shape[0], sall.shape[1]
-    NC, C = keep.shape[0], keep.shape[2]
-    half, mid = NC // 2, NS // 2
+    C = keep.shape[-1]
+    NC = w.shape[1] // C
+    mid, HALF, EVEN = NS // 2, SUB // 2, m1.shape[1]
+    ODD = NC - EVEN
 
     def peer(r):
         return lax.rem(i + r // 2, 2) * 2 + lax.rem(j + r % 2, 2)
@@ -100,15 +102,19 @@
     def _():
         pl.semaphore_wait(barrier, 4)
 
-    queries = {}
+    PIECES = 4
+    queries = []
     for r in (1, 2, 3):
-        rows = pl.ds(peer(r) * HD, HD)
-        queries[r] = remote(q_hbm.at[:, rows], qin.at[r], qs.at[r], qr.at[r], dp=peer(r))
-        queries[r].start()
+        pieces = PIECES if r == 3 else 1
+        for x in range(pieces):
+            tokens = pl.ds(x * (T // pieces), T // pieces)
+            source = q_hbm.at[tokens, pl.ds(peer(r) * HD, HD)]
+            n = r - 1 + x
+            queries.append(remote(source, qin.at[r, tokens], qs.at[n], qr.at[n], dp=peer(r)))
+    queries[0].start()
+    queries[1].start()
     own_query = pltpu.make_async_copy(q_hbm.at[:, pl.ds(d * HD, HD)], qin.at[0], lsem)
-    own_query.start()
     weights = pltpu.make_async_copy(w_hbm, w, wsem)
-    weights.start()
 
     def widen(src, dst, fn):
         step = 64
@@ -128,11 +134,13 @@
     def down(g):
         return remote(cb.at[g], cb.at[g], ds.at[g], cbr.at[g], sp=outer)
 
-    def spread(g):
-        n, x = lax.div(g, SUB), lax.rem(g, SUB)
-        r = lax.rem(n + 1, 4)
-        dd = lax.rem(i + lax.div(r, 2), 2) * 2 + lax.rem(j + lax.rem(r, 2), 2)
-        return remote(cb.at[g], sall.at[n, x], sts.at[g], str_.at[n, x], dp=dd)
+    def spread(n, x):
+        return remote(
+            cb.at[n * SUB + x], sall.at[n, x], sts.at[n, lax.rem(x, HALF)], str_.at[n, x], dp=peer((n + 1) % 4)
+        )
+
+    def forward(n, x, to):
+        return remote(sall.at[n, x], sall.at[n, x], fws.at[n, lax.rem(x, HALF)], str_.at[n, x], sp=to)
 
     for n in range(4):
         loads[n][0].wait()
@@ -156,9 +164,14 @@
             own[g, PART * size :] = masses
             up[g, PART * size :] = masses.astype(up.dtype)
 
-            @pl.when(has_inner)
-            def _():
-                up_end(g).start()
+            if n < 3:
+
+                @pl.when(has_inner)
+                def _():
+                    up_end(g).start()
+
+    own_query.start()
+    weights.start()
 
     def take_in(g):
         up_end(g).wait_recv()
@@ -167,34 +180,56 @@
         up[g] = total.astype(up.dtype)
         up_mid(g).start()
 
-    def finish(g):
-        up_mid(g).wait_recv()
+    LAG = 2
+
+    def reduce_states(n, begin=0, end=None):
+        end = SUB if end is None else end
 
         @pl.when(is_mid)
         def _():
-            cb[g] = (own[g] + cb[g].astype(jnp.float32)).astype(cb.dtype)
-
-        @pl.when(has_outer)
+            if n % 3 == 0 and begin == 0:
+                for x in range(LAG):
+                    take_in(n * SUB + x)
+
+            @pl.loop(begin, end)
+            def _(x):
+                g = n * SUB + x
+
+                @pl.when(x + LAG < (SUB if n > 1 else G))
+                def _():
+                    take_in(g + LAG)
+
+                up_mid(g).wait_recv()
+                cb[g] = (own[g] + cb[g].astype(jnp.float32)).astype(cb.dtype)
+
+                if n == 3:
+                    down(g).start()
+                else:
+
+                    @pl.when(x < HALF)
+                    def _():
+                        down(g).start()
+
+                    @pl.when(x >= HALF)
+                    def _():
+                        spread(n, x).start()
+
+        @pl.when(has_inner)
         def _():
-            down(g).start()
-
-    LAG = min(2, SUB)
-
-    def reduce_states(first, last, send):
-        @pl.when(is_mid)
-        def _():
-            for g in range(first, min(first + LAG, last)):
-                take_in(g)
-
-        @pl.loop(first, last)
-        def _(g):
-            @pl.when(jnp.logical_and(is_mid, g + LAG < last))
+            @pl.loop(begin, end if n == 3 else max(begin, min(end, HALF)))
+            def _(x):
+                up_mid(n * SUB + x).wait_recv()
+                if n < 3:
+                    spread(n, x).start()
+
+    def exchange(n):
+        for role, begin, to in ((has_inner, 0, center), (is_mid, HALF, outer)):
+
+            @pl.when(role)
             def _():
-                take_in(g + LAG)
-
-            finish(g)
-            if send:
-                spread(g).start()
+                for x in range(begin, begin + HALF):
+                    forward(n, x, to).wait_recv()
+                    forward(n, x, to).start()
 
     def query_features(r):
         widen(qin.at[r], wide, feature32)
@@ -213,11 +248,25 @@
             mixed[r, :, k * size : (k + 1) * size] = read.astype(mixed.dtype)
 
     def wait_spread(n):
-        for x in range(SUB):
-            remote(cb.at[0], sall.at[n, x], sts.at[0], str_.at[n, x], dp=d).wait_recv()
+        for role, begin, to in ((has_inner, HALF, center), (is_mid, 0, outer)):
+
+            @pl.when(role)
+            def _():
+                for x in range(begin, begin + HALF):
+                    forward(n, x, to).wait_recv()
 
     def columns(c, odd):
-        return pl.ds(pl.multiple_of((2 * c + odd) * C, C), C)
+        return pl.ds(pl.multiple_of((EVEN * odd + c) * C, C), C)
+
+    def every(body):
+        @pl.loop(0, ODD)
+        def _(c):
+            body(c, 0)
+            body(c, 1)
+
+        @pl.loop(ODD, EVEN)
+        def _(c):
+            body(c, 0)
 
     def first(c, odd, diagonal):
         return remote(
@@ -231,92 +280,116 @@
     def times(r, c, odd):
         return jnp.dot(mixed[r], w[:, columns(c, odd)], preferred_element_type=jnp.float32)
 
-    reduce_states(0, 3 * SUB, True)
-    for r in (1, 2):
-        queries[r].wait_recv()
-        query_features(r)
-    for r in (1, 2):
-        wait_spread(r - 1)
-        mix(r, lambda x: sall[r - 1, x])
+    def neighbour_messages(c, odd):
+        m1[odd, c, 0] = times(2 if odd else 1, c, odd).astype(m1.dtype)
+        first(c, odd, 0).start()
+
+    queries[2].start()
+    reduce_states(0)
+    queries[3].start()
+    queries[0].wait_recv()
+    query_features(1)
+    reduce_states(1)
+    exchange(0)
+    queries[4].start()
+    queries[1].wait_recv()
+    query_features(2)
+    reduce_states(2, 0, HALF)
+    exchange(1)
+    reduce_states(2, HALF)
+    queries[5].start()
+
+    @pl.when(has_inner)
+    def _():
+        for g in range(3 * SUB, G):
+            up_end(g).start()
+
     weights.wait()
-
-    @pl.loop(0, half)
+    wait_spread(0)
+    mix(1, lambda x: sall[0, x])
+    neighbour_messages(0, 0)
+    wait_spread(1)
+    mix(2, lambda x: sall[1, x])
+    neighbour_messages(0, 1)
+
+    @pl.loop(1, EVEN)
     def _(c):
-        for odd in range(2):
-            m1[odd, c, 0] = times(2 if odd else 1, c, odd).astype(m1.dtype)
-            first(c, odd, 0).start()
-
-    queries[3].wait_recv()
+        neighbour_messages(c, 0)
+
+        @pl.when(c < ODD)
+        def _():
+            neighbour_messages(c, 1)
+
+    exchange(2)
+    for x in range(PIECES):
+        queries[2 + x].wait_recv()
     query_features(3)
-    reduce_states(3 * SUB, 4 * SUB, False)
     wait_spread(2)
     mix(3, lambda x: sall[2, x])
 
-    @pl.loop(0, half)
-    def _(c):
-        for odd in range(2):
-            m1[odd, c, 1] = times(3, c, odd).astype(m1.dtype)
-            first(c, odd, 1).start()
-
+    @every
+    def diagonal_messages(c, odd):
+        m1[odd, c, 1] = times(3, c, odd).astype(m1.dtype)
+        first(c, odd, 1).start()
+
+    reduce_states(3)
     own_query.wait()
     query_features(0)
     mix(0, lambda x: cb[3 * SUB + x])
 
-    @pl.loop(0, half)
-    def _(c):
-        for odd in range(2):
-            block = times(0, c, odd)
-            first(c, odd, 0).wait_recv()
-            keep[2 * c + odd] = block + r1[odd, c, 0].astype(jnp.float32)
-
-    @pl.loop(0, half)
-    def _(c):
-        for odd in range(2):
-            block = times(1 if odd else 2, c, odd)
-            first(c, odd, 1).wait_recv()
-            s2[odd, c] = (block + r1[odd, c, 1].astype(jnp.float32)).astype(s2.dtype)
-            second(c, odd).start()
-
-    def leave(c, odd):
-        return pltpu.make_async_copy(outv.at[2 * c + odd], out_hbm.at[:, columns(c, odd)], osem.at[2 * c + odd])
-
-    @pl.loop(0, half)
-    def _(c):
-        for odd in range(2):
-            second(c, odd).wait_recv()
-            outv[2 * c + odd] = (keep[2 * c + odd] + r2[odd, c].astype(jnp.float32)).astype(outv.dtype)
-            leave(c, odd).start()
-
-    for r in (1, 2, 3):
-        queries[r].wait_send()
+    @every
+    def own_sums(c, odd):
+        block = times(0, c, odd)
+        first(c, odd, 0).wait_recv()
+        keep[odd, c] = block + r1[odd, c, 0].astype(jnp.float32)
+
+    @every
+    def second_messages(c, odd):
+        block = times(1 if odd else 2, c, odd)
+        first(c, odd, 1).wait_recv()
+        s2[odd, c] = (block + r1[odd, c, 1].astype(jnp.float32)).astype(s2.dtype)
+        second(c, odd).start()
+
+    @every
+    def last_sums(c, odd):
+        second(c, odd).wait_recv()
+        out_hbm[:, columns(c, odd)] = (keep[odd, c] + r2[odd, c].astype(jnp.float32)).astype(out_hbm.dtype)
+
+    for query in queries:
+        query.wait_send()
 
     @pl.loop(0, G)
     def _(g):
         up_end(g).wait_send()
 
-        @pl.when(has_outer)
+    for role, begin, to in ((has_inner, 0, center), (is_mid, HALF, outer)):
+
+        @pl.when(role)
         def _():
-            down(g).wait_send()
-
-    @pl.loop(0, 3 * SUB)
-    def _(g):
-        spread(g).wait_send()
-
-    @pl.loop(0, half)
-    def _(c):
-        for odd in range(2):
-            first(c, odd, 0).wait_send()
-            first(c, odd, 1).wait_send()
-            second(c, odd).wait_send()
-            leave(c, odd).wait()
+            for n in range(3):
+                for x in range(begin, begin + HALF):
+                    spread(n, x).wait_send()
+                    forward(n, x, to).wait_send()
+
+    @pl.when(has_outer)
+    def _():
+        for n in range(4):
+            for x in range(SUB if n == 3 else HALF):
+                down(n * SUB + x).wait_send()
+
+    @every
+    def drain(c, odd):
+        first(c, odd, 0).wait_send()
+        first(c, odd, 1).wait_send()
+        second(c, odd).wait_send()
 
 
 def kernel_body(query_rows, key_rows, value_rows, out_weight):
     NS = lax.axis_size("sp")
     _, T, H, size = query_rows.shape
     V, rows = out_weight.shape[1], out_weight.shape[0]
-    HD, NC = H // 4, 16
-    C, half, count = V // NC, NC // 2, T * NS
+    HD, NC, EVEN = H // 4, 16, 8
+    C, count = V // NC, T * NS
     SUB = HD // PART
     G, R = 4 * SUB, PART * size + EXTRA
     bf, f32 = jnp.bfloat16, jnp.float32
@@ -326,7 +399,7 @@
         functools.partial(kernel, NS, count),
         out_shape=jax.ShapeDtypeStruct((T, V), bf),
         in_specs=[hbm] * 4,
-        out_specs=hbm,
+        out_specs=pl.BlockSpec(memory_space=pltpu.VMEM),
         scratch_shapes=[
             pltpu.VMEM((4, T, HD, size), bf),
             pltpu.VMEM((4, T, HD, size), bf),
@@ -341,18 +414,17 @@
             pltpu.VMEM((3, SUB, R, size), bf),
             pltpu.VMEM((4, HD, T, size), bf),
             pltpu.VMEM((4, T, rows), bf),
-            pltpu.VMEM((2, half, 2, T, C), bf),
-            pltpu.VMEM((2, half, 2, T, C), bf),
-            pltpu.VMEM((2, half, T, C), bf),
-            pltpu.VMEM((2, half, T, C), bf),
-            pltpu.VMEM((NC, T, C), f32),
-            pltpu.VMEM((NC, T, C), bf),
-            dma((4,)), dma((4,)), dma, dma, dma((NC,)), dma((4,)), dma((4,)),
-            dma((G,)), dma((G,)), dma((G,)), dma((G,)), dma((3 * SUB,)), dma((3, SUB)),
-            dma((2, half, 2)), dma((2, half, 2)), dma((2, half)), dma((2, half)),
+            pltpu.VMEM((2, EVEN, 2, T, C), bf),
+            pltpu.VMEM((2, EVEN, 2, T, C), bf),
+            pltpu.VMEM((2, EVEN, T, C), bf),
+            pltpu.VMEM((2, EVEN, T, C), bf),
+            pltpu.VMEM((2, EVEN, T, C), f32),
+            dma((4,)), dma((4,)), dma, dma, dma((6,)), dma((6,)),
+            dma((G,)), dma((G,)), dma((G,)), dma((G,)), dma((3, SUB // 2)), dma((3, SUB // 2)), dma((3, SUB)),
+            dma((2, EVEN, 2)), dma((2, EVEN, 2)), dma((2, EVEN)), dma((2, EVEN)),
         ],
         compiler_params=pltpu.CompilerParams(
-            collective_id=0, has_side_effects=True, vmem_limit_bytes=60 * 2**20
+            collective_id=0, has_side_effects=True, vmem_limit_bytes=50 * 2**20
         ),
     )(query_rows[0], key_rows[0], value_rows[0], out_weight)
     return out[None]

time: 113 us -> 109 us (0.965)
  Pallas kernels: 110 us -> 108 us
  local copies, waits for them, and re-layouts: 3.13 us -> 1.32 us
    pallas_call x1, Pallas kernels: 110 us -> 108 us  [kernel_body(): pl.pallas_call(functools.partial(kernel, NS, count), out_shape=jax.ShapeD...]
    unnamed x1, local copies, waits for them, and re-layouts: 3.13 us -> 1.32 us
where the time goes in v2:
time: 109 us
  Pallas kernels  108 us (99%)
  local copies, waits for them, and re-layouts  1.32 us (1%)
    pallas_call x1, Pallas kernels, kernel_body(): pl.pallas_call(functools.partial(kernel, NS, count), out_shape=jax.ShapeD...  108 us

profile of v2, /device:TPU:0, one launch (start us, length us, event | category | flops | bytes accessed | tf_op | source)
XLA Modules:
  0.0 108.9 jit_solution(14931265343732371081)
XLA Ops:
  0.0 107.6 %shard_map.46 = bf16[256,4096]{1,0:T(8,128)(2,1)S(1)} custom-call(bf16[256,32,128]{2,1,0:T(8,128)(2,1)} %bitcast.5, bf16[256,32,128]{2,1,0:T(8,128)(2,1)} %bitcast.6, bf16[256,32,128]{2,1,0:T(8,128)(2,1)} %bitcast.7, bf16[1024,4096]{1,0:T(8,128)(2,1)} %w_hbm.1), custom_call_target="tpu_custom_call" | custom-call | tf_op jit(solution)/shard_map/pallas_call | solution.py:398
  107.6 1.3 %copy.6 = bf16[1,256,4096]{2,1,0:T(8,128)(2,1)} copy(bf16[1,256,4096]{2,1,0:T(8,128)(2,1)S(1)} %bitcast.4) | data formatting | bytes 4194304

commit v3 on v1

v3 whole, which is shorter than its diff:
```python
import functools

import jax
import jax.numpy as jnp
from jax import lax
from jax.experimental import pallas as pl
from jax.experimental.pallas import tpu as pltpu
from jax.sharding import PartitionSpec as P


def feature_map(values):
    wide = values.astype(jnp.float32)
    return jnp.where(wide > 0.0, wide + 1.0, jnp.exp(jnp.minimum(wide, 0.0))).astype(jnp.bfloat16)


def plain_body(query_rows, key_rows, value_rows, out_weight):
    query_feature, key_feature = (feature_map(query_rows), feature_map(key_rows))
    count = query_rows.shape[1] * lax.axis_size("sp")
    state = (
        jnp.einsum("bthd,bthe->bhde", key_feature, value_rows, preferred_element_type=jnp.float32)
        / count
    )
    mass = jnp.sum(key_feature.astype(jnp.float32), axis=1) / count
    state = lax.psum(state.astype(jnp.bfloat16), "sp")
    mass = lax.psum(mass, "sp")
    top = jnp.einsum("bthd,bhde->bthe", query_feature, state, preferred_element_type=jnp.float32)
    bottom = jnp.einsum(
        "bthd,bhd->bth", query_feature.astype(jnp.float32), mass, precision=lax.Precision.HIGHEST
    )
    mixed = (top / (bottom + 0.001)[..., None] * count**0.5).astype(jnp.bfloat16)
    mixed = mixed.reshape(mixed.shape[0], mixed.shape[1], -1)
    mine = lax.all_to_all(mixed, "dp", split_axis=2, concat_axis=0, tiled=True)
    part = jnp.einsum("btw,wv->btv", mine, out_weight, preferred_element_type=jnp.float32)
    return lax.psum_scatter(part.astype(jnp.bfloat16), "dp", scatter_dimension=0, tiled=True)


MESH = pl.DeviceIdType.MESH
NT = (((1,), (1,)), ((), ()))
TN = (((0,), (0,)), ((), ()))
EXTRA = 16
PART = 2


def feature32(values):
    wide = values.astype(jnp.float32)
    return jnp.where(wide > 0.0, wide + 1.0, jnp.exp(jnp.minimum(wide, 0.0)))


def remote(src, dst, send, recv, **where):
    return pltpu.make_async_remote_copy(
        src_ref=src, dst_ref=dst, send_sem=send, recv_sem=recv, device_id=where, device_id_type=MESH
    )


def kernel(
    NS, count, q_hbm, k_hbm, v_hbm, w_hbm, out_ref,
    kv, qin, wide, wide2, w, own, up, inb, cb, sall, qf, mixed,
    m1, r1, s2, r2, keep,
    ksem, lsem, wsem, qs, qr, us, inr, cbr, ds, sts, fws, str_, s1, t1, s2s, s2r,
):
    d, p = lax.axis_index("dp"), lax.axis_index("sp")
    i, j = lax.div(d, 2), lax.rem(d, 2)
    T, HD, size = qin.shape[1:]
    G, SUB = up.shape[0], sall.shape[1]
    C = keep.shape[-1]
    NC = w.shape[1] // C
    mid, half = NS // 2, NC // 2

    def peer(r):
        return lax.rem(i + r // 2, 2) * 2 + lax.rem(j + r % 2, 2)

    side = 1 - lax.div(p, mid)
    center = p - 1 + 2 * side
    outer = p + 1 - 2 * side
    is_mid = jnp.logical_or(p == mid - 1, p == mid)
    has_outer = jnp.logical_and(p > 0, p < NS - 1)
    has_inner = jnp.logical_not(is_mid)
    inside = lax.div(lax.rem(p, NS - 1) + 1, 2)
    mine = inside * (p + 1) + (1 - inside) * lax.div(p, NS - 1)

    for n in range(4):
        rows = pl.ds(peer((n + 1) % 4) * HD, HD)
        pltpu.make_async_copy(k_hbm.at[:, rows], kv.at[n, 0], ksem.at[n]).start()
        pltpu.make_async_copy(v_hbm.at[:, rows], kv.at[n, 1], ksem.at[n]).start()

    barrier = pltpu.get_barrier_semaphore()
    for r in (1, 2, 3):
        pl.semaphore_signal(barrier, inc=1, device_id={"dp": peer(r)}, device_id_type=MESH)
    for x in range(1, NS):
        pl.semaphore_signal(barrier, inc=1, device_id={"sp": lax.rem(p + x, NS)}, device_id_type=MESH)
    pl.semaphore_wait(barrier, 2 + NS)

    PIECES, FIRST, DELAY = 8, 3, 1
    def piece(k):
        tokens = pl.ds(pl.multiple_of(k * (T // PIECES), T // PIECES), T // PIECES)
        source = q_hbm.at[tokens, pl.ds(peer(3) * HD, HD)]
        return remote(source, qin.at[3, tokens], qs, qr.at[2], dp=peer(3))

    queries = {}
    for r in (1, 2):
        source = q_hbm.at[:, pl.ds(peer(r) * HD, HD)]
        queries[r] = remote(source, qin.at[r], qs, qr.at[r - 1], dp=peer(r))
        queries[r].start()
    own_query = pltpu.make_async_copy(q_hbm.at[:, pl.ds(d * HD, HD)], qin.at[0], lsem)
    for k in range(FIRST):
        piece(k).start()
    weights = pltpu.make_async_copy(w_hbm, w, wsem)

    def widen(src, dst, fn):
        step = 64

        @pl.loop(0, T // step)
        def _(x):
            block = fn(src[pl.ds(pl.multiple_of(x * step, step), step)])
            rows = step * HD
            dst[pl.ds(pl.multiple_of(x * rows, rows), rows)] = block.reshape(rows, size)

    def place(k):
        return (k % 2) * SUB + k // 2

    def up_end(g):
        return remote(up.at[g], inb.at[g], us, inr.at[g], sp=center)

    def up_mid(g):
        return remote(up.at[g], cb.at[g], us, cbr.at[g], sp=center)

    def down(g):
        return remote(cb.at[g], cb.at[g], ds, cbr.at[g], sp=outer)

    def spread(n, x):
        r = n + 1
        dd = (i + r // 2) % 2 * 2 + (j + r) % 2
        return remote(cb.at[n * SUB + x], sall.at[n, x], sts, str_.at[n, x], dp=dd)

    def forward(x):
        return remote(sall.at[2, mine], sall.at[2, mine], fws, str_.at[2, mine], sp=lax.rem(p + x, NS))

    for n in range(4):
        pltpu.make_async_copy(kv.at[n], kv.at[n], ksem.at[n]).wait()
        widen(kv.at[n, 0], wide, feature32)
        widen(kv.at[n, 1], wide2, lambda x: x.astype(jnp.float32))

        @pl.loop(0, SUB)
        def _(x):
            g = n * SUB + x
            row = lax.broadcasted_iota(jnp.int32, (EXTRA, size), 0)
            masses = jnp.zeros((EXTRA, size), jnp.float32)
            for k in range(PART):
                key = wide[pl.ds(x * PART + k, T, stride=HD), :].astype(jnp.bfloat16)
                value = wide2[pl.ds(x * PART + k, T, stride=HD), :].astype(jnp.bfloat16)
                state = lax.dot_general(value, key, TN, preferred_element_type=jnp.float32) / count
                mass = jnp.sum(key.astype(jnp.float32), axis=0, keepdims=True) / count
                masses = jnp.where(row == k, mass, masses)
                own[g, k * size : (k + 1) * size] = state
                up[g, k * size : (k + 1) * size] = state.astype(up.dtype)
            own[g, PART * size :] = masses
            up[g, PART * size :] = masses.astype(up.dtype)

        @pl.when(has_inner)
        def _():
            if n == 0:
                up_end(0).start()
            if n == 1:
                for k in range(1, 2 * SUB):
                    up_end(place(k)).start()
            if n == 2:
                for g in range(2 * SUB, 3 * SUB):
                    up_end(g).start()

    own_query.start()
    weights.start()

    def take_in(g, both):
        up_end(g).wait_recv()
        total = own[g] + inb[g].astype(jnp.float32)
        keeps = lax.rem(g, 2) == p - 1

        def hold():
            own[g] = total

        def send():
            up[g] = total.astype(up.dtype)
            up_mid(g).start()

        if both:
            hold()
            send()
        else:
            pl.when(keeps)(hold)
            pl.when(jnp.logical_not(keeps))(send)

    def finish(g):
        up_mid(g).wait_recv()
        cb[g] = (own[g] + cb[g].astype(jnp.float32)).astype(cb.dtype)

    LAG = 2

    def reduce_neighbours():
        def step(k):
            n, x = k % 2, k // 2
            spread(n, x).start()

            @pl.when(k >= FIRST + DELAY)
            def _():
                piece(k - DELAY).start()

        @pl.when(is_mid)
        def _():
            for k in range(LAG):
                take_in(place(k), True)

            @pl.loop(0, 2 * SUB)
            def _(k):
                @pl.when(k + LAG < 2 * SUB)
                def _():
                    take_in(place(k + LAG), True)

                finish(place(k))
                down(place(k)).start()
                step(k)

        @pl.when(has_inner)
        def _():
            @pl.loop(0, 2 * SUB)
            def _(k):
                up_mid(place(k)).wait_recv()
                step(k)

    def reduce_diagonal():
        @pl.when(is_mid)
        def _():
            @pl.loop(2 * SUB, 3 * SUB)
            def _(g):
                take_in(g, False)

            for x in range(2):
                g = 2 * SUB + 2 * x + p - 1
                finish(g)
                if x == 0:
                    down(g).start()

        @pl.when(has_inner)
        def _():
            up_mid(2 * SUB + mine).wait_recv()

        spread(2, mine).start()

    def reduce_own():
        @pl.when(is_mid)
        def _():
            @pl.loop(3 * SUB, G)
            def _(g):
                take_in(g, True)

            @pl.loop(3 * SUB, G)
            def _(g):
                finish(g)
                down(g).start()

        @pl.when(has_inner)
        def _():
            @pl.loop(3 * SUB, G)
            def _(g):
                up_mid(g).wait_recv()

    def exchange():
        forward(1).wait_recv()
        for x in range(1, NS):
            forward(x).start()

    def query_features(r):
        widen(qin.at[r], wide, feature32)
        for k in range(HD):
            qf[r, k] = wide[pl.ds(k, T, stride=HD), :].astype(qf.dtype)

    def mix(r, states):
        for k in range(HD):
            x, kk = k // PART, k % PART
            block = states(x)
            masses = block[PART * size :].astype(jnp.float32)
            mass = jnp.broadcast_to(masses[kk : kk + 1], (size, size)).astype(jnp.bfloat16)
            both = jnp.concatenate([block[kk * size : (kk + 1) * size], mass], axis=0)
            read = lax.dot_general(qf[r, k], both, NT, preferred_element_type=jnp.float32)
            read = read[:, :size] / (read[:, size:] + 0.001) * count**0.5
            mixed[r, :, k * size : (k + 1) * size] = read.astype(mixed.dtype)

    def wait_spread(n):
        for x in range(SUB):

            def wait():
                spread(n, x).wait_recv()

            if n < 2:
                wait()
            else:
                pl.when(x != mine)(wait)

    def columns(c, odd):
        return pl.ds(pl.multiple_of((2 * c + odd) * C, C), C)

    def first(c, odd, diagonal):
        recv = t1.at[2 + c] if diagonal else t1.at[odd]
        return remote(
            m1.at[diagonal, c, odd], r1.at[diagonal, c, odd], s1, recv, dp=peer(2 if odd else 1)
        )

    def second(c, odd):
        return remote(s2.at[c, odd], r2.at[c, odd], s2s, s2r.at[c], dp=peer(1 if odd else 2))

    def arrived(ref, semaphore):
        pltpu.make_async_copy(ref, ref, semaphore).wait()

    def times(r, c, odd):
        return jnp.dot(mixed[r], w[:, columns(c, odd)], preferred_element_type=jnp.float32)

    def neighbour_messages(c, odd):
        m1[0, c, odd] = times(2 if odd else 1, c, odd).astype(m1.dtype)
        first(c, odd, 0).start()

    reduce_neighbours()
    for k in range(2 * SUB - DELAY, PIECES):
        piece(k).start()
    for r in (1, 2):
        queries[r].wait_recv()
        query_features(r)
    reduce_diagonal()
    weights.wait()
    wait_spread(0)
    mix(1, lambda x: sall[0, x])
    neighbour_messages(0, 0)
    wait_spread(1)
    mix(2, lambda x: sall[1, x])
    neighbour_messages(0, 1)

    @pl.when(has_inner)
    def _():
        for g in range(3 * SUB, G):
            up_end(g).start()

    @pl.loop(1, half)
    def _(c):
        for odd in range(2):
            neighbour_messages(c, odd)

    exchange()
    arrived(qin.at[3], qr.at[2])
    query_features(3)
    wait_spread(2)
    mix(3, lambda x: sall[2, x])

    @pl.loop(0, half)
    def _(c):
        for odd in range(2):
            m1[1, c, odd] = times(3, c, odd).astype(m1.dtype)
            first(c, odd, 1).start()

    reduce_own()
    own_query.wait()
    query_features(0)
    mix(0, lambda x: cb[3 * SUB + x])

    for odd in range(2):
        arrived(s2.at[:, odd], t1.at[odd])

    @pl.loop(0, half)
    def _(c):
        for odd in range(2):
            keep[c, odd] = times(0, c, odd) + r1[0, c, odd].astype(jnp.float32)

    @pl.loop(0, half)
    def _(c):
        blocks = [times(1 if odd else 2, c, odd) for odd in range(2)]
        arrived(r1.at[1, c], t1.at[2 + c])
        for odd in range(2):
            s2[c, odd] = (blocks[odd] + r1[1, c, odd].astype(jnp.float32)).astype(s2.dtype)
            second(c, odd).start()

    @pl.loop(0, half)
    def _(c):
        arrived(r2.at[c], s2r.at[c])
        for odd in range(2):
            total = keep[c, odd] + r2[c, odd].astype(jnp.float32)
            out_ref[:, columns(c, odd)] = total.astype(out_ref.dtype)

    arrived(qin.at[pl.ds(0, 3)], qs)
    arrived(up.at[pl.ds(0, 2 * SUB + 1)], sts)
    arrived(up.at[pl.ds(0, NS - 1)], fws)
    arrived(m1, s1)
    arrived(s2, s2s)

    @pl.when(has_inner)
    def _():
        arrived(up, us)

    @pl.when(is_mid)
    def _():
        arrived(up.at[pl.ds(0, 3 * SUB + 2)], us)
        arrived(up.at[pl.ds(0, 3 * SUB + 1)], ds)


def kernel_body(query_rows, key_rows, value_rows, out_weight):
    NS = lax.axis_size("sp")
    _, T, H, size = query_rows.shape
    V, rows = out_weight.shape[1], out_weight.shape[0]
    HD, NC = H // 4, 16
    C, half, count = V // NC, NC // 2, T * NS
    SUB = HD // PART
    G, R = 4 * SUB, PART * size + EXTRA
    bf, f32 = jnp.bfloat16, jnp.float32
    dma = pltpu.SemaphoreType.DMA
    hbm = pl.BlockSpec(memory_space=pl.ANY)
    out = pl.pallas_call(
        functools.partial(kernel, NS, count),
        out_shape=jax.ShapeDtypeStruct((T, V), bf),
        in_specs=[hbm] * 4,
        out_specs=pl.BlockSpec(memory_space=pltpu.VMEM),
        scratch_shapes=[
            pltpu.VMEM((4, 2, T, HD, size), bf),
            pltpu.VMEM((4, T, HD, size), bf),
            pltpu.VMEM((T * HD, size), f32),
            pltpu.VMEM((T * HD, size), f32),
            pltpu.VMEM((rows, V), bf),
            pltpu.VMEM((G, R, size), f32),
            pltpu.VMEM((G, R, size), bf),
            pltpu.VMEM((G, R, size), bf),
            pltpu.VMEM((G, R, size), bf),
            pltpu.VMEM((3, SUB, R, size), bf),
            pltpu.VMEM((4, HD, T, size), bf),
            pltpu.VMEM((4, T, rows), bf),
            pltpu.VMEM((2, half, 2, T, C), bf),
            pltpu.VMEM((2, half, 2, T, C), bf),
            pltpu.VMEM((half, 2, T, C), bf),
            pltpu.VMEM((half, 2, T, C), bf),
            pltpu.VMEM((half, 2, T, C), f32),
            dma((4,)), dma, dma, dma, dma((3,)),
            dma, dma((G,)), dma((G,)), dma, dma, dma, dma((3, SUB)),
            dma, dma((2 + half,)), dma, dma((half,)),
        ],
        compiler_params=pltpu.CompilerParams(
            collective_id=0, has_side_effects=True, vmem_limit_bytes=50 * 2**20
        ),
    )(query_rows[0], key_rows[0], value_rows[0], out_weight)
    return out[None]


def split_of(n):
    for a in range(int(n**0.5), 0, -1):
        if n % a == 0:
            return a, n // a


def body(query_rows, key_rows, value_rows, out_weight):
    ND, NS = lax.axis_size("dp"), lax.axis_size("sp")
    batch, T, H, size = query_rows.shape
    rows, V = out_weight.shape
    fits = batch == 1 and split_of(ND) == (2, 2) and NS == 4 and H // 4 == 4 * PART
    fits = fits and size == 128 and T % 64 == 0 and V % 4096 == 0 and rows * 4 == H * size
    need = 2 * rows * V + 18 * T * V + 12 * T * H * size + 14 * H * size * size
    run = kernel_body if fits and need < 50 * 2**20 else plain_body
    return run(query_rows, key_rows, value_rows, out_weight)


def solution(mesh):
    placed = (
        P(("shift", "dp"), "sp", None, None),
        P(("shift", "dp"), "sp", None, None),
        P(("shift", "dp"), "sp", None, None),
        P(("shift", "dp"), None),
    )
    return jax.shard_map(
        body, mesh=mesh, in_specs=placed, out_specs=P(("shift", "dp"), "sp", None), check_vma=False
    )
```

time: 113 us -> 108 us (0.956)
  Pallas kernels: 110 us -> 106 us
  local copies, waits for them, and re-layouts: 3.13 us -> 1.32 us
    pallas_call x1, Pallas kernels: 110 us -> 106 us  [kernel_body(): pl.pallas_call(functools.partial(kernel, NS, count), out_shape=jax.ShapeD...]
    unnamed x1, local copies, waits for them, and re-layouts: 3.13 us -> 1.32 us
where the time goes in v3:
time: 108 us
  Pallas kernels  106 us (98%)
  local copies, waits for them, and re-layouts  1.32 us (1%)
    pallas_call x1, Pallas kernels, kernel_body(): pl.pallas_call(functools.partial(kernel, NS, count), out_shape=jax.ShapeD...  106 us

profile of v3, /device:TPU:0, one launch (start us, length us, event | category | flops | bytes accessed | tf_op | source)
XLA Modules:
  0.0 107.6 jit_solution(5409881742297474439)
XLA Ops:
  0.0 106.3 %shard_map.46 = bf16[256,4096]{1,0:T(8,128)(2,1)S(1)} custom-call(bf16[256,32,128]{2,1,0:T(8,128)(2,1)} %bitcast.5, bf16[256,32,128]{2,1,0:T(8,128)(2,1)} %bitcast.6, bf16[256,32,128]{2,1,0:T(8,128)(2,1)} %bitcast.7, bf16[1024,4096]{1,0:T(8,128)(2,1)} %w_hbm.1), custom_call_target="tpu_custom_call" | custom-call | tf_op jit(solution)/shard_map/pallas_call | solution.py:412
  106.3 1.3 %copy.6 = bf16[1,256,4096]{2,1,0:T(8,128)(2,1)} copy(bf16[1,256,4096]{2,1,0:T(8,128)(2,1)S(1)} %bitcast.4) | data formatting | bytes 4194304

commit v4 on v3

--- a/solution.py
+++ b/solution.py
@@ -88,9 +88,8 @@
         pl.semaphore_signal(barrier, inc=1, device_id={"dp": peer(r)}, device_id_type=MESH)
     for x in range(1, NS):
         pl.semaphore_signal(barrier, inc=1, device_id={"sp": lax.rem(p + x, NS)}, device_id_type=MESH)
-    pl.semaphore_wait(barrier, 2 + NS)
-
-    PIECES, FIRST, DELAY = 8, 3, 1
+    PIECES, FIRST = 8, 3
+
     def piece(k):
         tokens = pl.ds(pl.multiple_of(k * (T // PIECES), T // PIECES), T // PIECES)
         source = q_hbm.at[tokens, pl.ds(peer(3) * HD, HD)]
@@ -100,10 +99,7 @@
     for r in (1, 2):
         source = q_hbm.at[:, pl.ds(peer(r) * HD, HD)]
         queries[r] = remote(source, qin.at[r], qs, qr.at[r - 1], dp=peer(r))
-        queries[r].start()
     own_query = pltpu.make_async_copy(q_hbm.at[:, pl.ds(d * HD, HD)], qin.at[0], lsem)
-    for k in range(FIRST):
-        piece(k).start()
     weights = pltpu.make_async_copy(w_hbm, w, wsem)
 
     def widen(src, dst, fn):
@@ -132,6 +128,9 @@
         dd = (i + r // 2) % 2 * 2 + (j + r) % 2
         return remote(cb.at[n * SUB + x], sall.at[n, x], sts, str_.at[n, x], dp=dd)
 
+    def relay(n, x, to):
+        return remote(sall.at[n, x], sall.at[n, x], fws, str_.at[n, x], sp=to)
+
     def forward(x):
         return remote(sall.at[2, mine], sall.at[2, mine], fws, str_.at[2, mine], sp=lax.rem(p + x, NS))
 
@@ -139,6 +138,13 @@
         pltpu.make_async_copy(kv.at[n], kv.at[n], ksem.at[n]).wait()
         widen(kv.at[n, 0], wide, feature32)
         widen(kv.at[n, 1], wide2, lambda x: x.astype(jnp.float32))
+
+        if n == 0:
+            pl.semaphore_wait(barrier, 2 + NS)
+            for r in (1, 2):
+                queries[r].start()
+            for k in range(FIRST):
+                piece(k).start()
 
         @pl.loop(0, SUB)
         def _(x):
@@ -163,10 +169,6 @@
             if n == 1:
                 for k in range(1, 2 * SUB):
                     up_end(place(k)).start()
-            if n == 2:
-                for g in range(2 * SUB, 3 * SUB):
-                    up_end(g).start()
-
     own_query.start()
     weights.start()
 
@@ -196,13 +198,9 @@
     LAG = 2
 
     def reduce_neighbours():
-        def step(k):
-            n, x = k % 2, k // 2
-            spread(n, x).start()
-
-            @pl.when(k >= FIRST + DELAY)
-            def _():
-                piece(k - DELAY).start()
+        def step(t, k):
+            spread(k % 2, k // 2).start()
+            piece(FIRST + t).start()
 
         @pl.when(is_mid)
         def _():
@@ -216,23 +214,42 @@
                     take_in(place(k + LAG), True)
 
                 finish(place(k))
-                down(place(k)).start()
-                step(k)
+
+                @pl.when(k < SUB)
+                def _():
+                    down(place(k)).start()
+
+                @pl.when(k >= SUB)
+                def _():
+                    step(k - SUB, k)
 
         @pl.when(has_inner)
         def _():
-            @pl.loop(0, 2 * SUB)
+            @pl.loop(0, SUB)
             def _(k):
                 up_mid(place(k)).wait_recv()
-                step(k)
-
-    def reduce_diagonal():
+                step(k, k)
+
+    def swap_halves():
+        for role, begin, to in ((has_inner, 0, center), (is_mid, SUB, outer)):
+
+            @pl.when(role)
+            def _():
+                @pl.loop(begin, begin + SUB)
+                def _(k):
+                    relay(k % 2, k // 2, to).wait_recv()
+                    relay(k % 2, k // 2, to).start()
+
+    def take_diagonal():
         @pl.when(is_mid)
         def _():
             @pl.loop(2 * SUB, 3 * SUB)
             def _(g):
                 take_in(g, False)
 
+    def reduce_diagonal():
+        @pl.when(is_mid)
+        def _():
             for x in range(2):
                 g = 2 * SUB + 2 * x + p - 1
                 finish(g)
@@ -244,6 +261,12 @@
             up_mid(2 * SUB + mine).wait_recv()
 
         spread(2, mine).start()
+
+    def send_states(n):
+        @pl.when(has_inner)
+        def _():
+            for g in range(n * SUB, n * SUB + SUB):
+                up_end(g).start()
 
     def reduce_own():
         @pl.when(is_mid)
@@ -286,14 +309,14 @@
 
     def wait_spread(n):
         for x in range(SUB):
-
-            def wait():
+            if n < 2:
+                away = is_mid if x < 2 else has_inner
+            else:
+                away = x != mine
+
+            @pl.when(away)
+            def _():
                 spread(n, x).wait_recv()
-
-            if n < 2:
-                wait()
-            else:
-                pl.when(x != mine)(wait)
 
     def columns(c, odd):
         return pl.ds(pl.multiple_of((2 * c + odd) * C, C), C)
@@ -318,12 +341,14 @@
         first(c, odd, 0).start()
 
     reduce_neighbours()
-    for k in range(2 * SUB - DELAY, PIECES):
+    for k in range(FIRST + SUB, PIECES):
         piece(k).start()
-    for r in (1, 2):
-        queries[r].wait_recv()
-        query_features(r)
-    reduce_diagonal()
+    queries[1].wait_recv()
+    query_features(1)
+    swap_halves()
+    send_states(2)
+    queries[2].wait_recv()
+    query_features(2)
     weights.wait()
     wait_spread(0)
     mix(1, lambda x: sall[0, x])
@@ -332,12 +357,16 @@
     mix(2, lambda x: sall[1, x])
     neighbour_messages(0, 1)
 
-    @pl.when(has_inner)
-    def _():
-        for g in range(3 * SUB, G):
-            up_end(g).start()
-
-    @pl.loop(1, half)
+    @pl.loop(1, 4)
+    def _(c):
+        for odd in range(2):
+            neighbour_messages(c, odd)
+
+    take_diagonal()
+    reduce_diagonal()
+    send_states(3)
+
+    @pl.loop(4, half)
     def _(c):
         for odd in range(2):
             neighbour_messages(c, odd)
@@ -383,8 +412,8 @@
             out_ref[:, columns(c, odd)] = total.astype(out_ref.dtype)
 
     arrived(qin.at[pl.ds(0, 3)], qs)
-    arrived(up.at[pl.ds(0, 2 * SUB + 1)], sts)
-    arrived(up.at[pl.ds(0, NS - 1)], fws)
+    arrived(up.at[pl.ds(0, SUB + 1)], sts)
+    arrived(up.at[pl.ds(0, SUB + NS - 1)], fws)
     arrived(m1, s1)
     arrived(s2, s2s)
 
@@ -395,7 +424,7 @@
     @pl.when(is_mid)
     def _():
         arrived(up.at[pl.ds(0, 3 * SUB + 2)], us)
-        arrived(up.at[pl.ds(0, 3 * SUB + 1)], ds)
+        arrived(up.at[pl.ds(0, 2 * SUB + 1)], ds)
 
 
 def kernel_body(query_rows, key_rows, value_rows, out_weight):

time: 108 us -> 106 us (0.981)
  Pallas kernels: 106 us -> 104 us
    pallas_call x1, Pallas kernels: 106 us -> 104 us  [kernel_body(): pl.pallas_call(functools.partial(kernel, NS, count), out_shape=jax.ShapeD...]
where the time goes in v4:
time: 106 us
  Pallas kernels  104 us (98%)
  local copies, waits for them, and re-layouts  1.32 us (1%)
    pallas_call x1, Pallas kernels, kernel_body(): pl.pallas_call(functools.partial(kernel, NS, count), out_shape=jax.ShapeD...  104 us

profile of v4, /device:TPU:0, one launch (start us, length us, event | category | flops | bytes accessed | tf_op | source)
XLA Modules:
  0.0 105.7 jit_solution(495171955626429971)
XLA Ops:
  0.0 104.4 %shard_map.46 = bf16[256,4096]{1,0:T(8,128)(2,1)S(1)} custom-call(bf16[256,32,128]{2,1,0:T(8,128)(2,1)} %bitcast.5, bf16[256,32,128]{2,1,0:T(8,128)(2,1)} %bitcast.6, bf16[256,32,128]{2,1,0:T(8,128)(2,1)} %bitcast.7, bf16[1024,4096]{1,0:T(8,128)(2,1)} %w_hbm.1), custom_call_target="tpu_custom_call" | custom-call | tf_op jit(solution)/shard_map/pallas_call | solution.py:441
  104.4 1.3 %copy.6 = bf16[1,256,4096]{2,1,0:T(8,128)(2,1)} copy(bf16[1,256,4096]{2,1,0:T(8,128)(2,1)S(1)} %bitcast.4) | data formatting | bytes 4194304

commit v5 on v4

--- a/solution.py
+++ b/solution.py
@@ -357,12 +357,14 @@
     mix(2, lambda x: sall[1, x])
     neighbour_messages(0, 1)
 
-    @pl.loop(1, 4)
+    @pl.loop(1, 3)
     def _(c):
         for odd in range(2):
             neighbour_messages(c, odd)
 
     take_diagonal()
+    neighbour_messages(3, 0)
+    neighbour_messages(3, 1)
     reduce_diagonal()
     send_states(3)
 

time: 106 us -> 106 us (level)
  no operation moved by 1% of the time
where the time goes in v5:
time: 106 us
  Pallas kernels  104 us (98%)
  local copies, waits for them, and re-layouts  1.32 us (1%)
    pallas_call x1, Pallas kernels, kernel_body(): pl.pallas_call(functools.partial(kernel, NS, count), out_shape=jax.ShapeD...  104 us

profile of v5, /device:TPU:0, one launch (start us, length us, event | category | flops | bytes accessed | tf_op | source)
XLA Modules:
  0.0 105.7 jit_solution(4788039261699302560)
XLA Ops:
  0.0 104.4 %shard_map.46 = bf16[256,4096]{1,0:T(8,128)(2,1)S(1)} custom-call(bf16[256,32,128]{2,1,0:T(8,128)(2,1)} %bitcast.5, bf16[256,32,128]{2,1,0:T(8,128)(2,1)} %bitcast.6, bf16[256,32,128]{2,1,0:T(8,128)(2,1)} %bitcast.7, bf16[1024,4096]{1,0:T(8,128)(2,1)} %w_hbm.1), custom_call_target="tpu_custom_call" | custom-call | tf_op jit(solution)/shard_map/pallas_call | solution.py:443
  104.4 1.3 %copy.6 = bf16[1,256,4096]{2,1,0:T(8,128)(2,1)} copy(bf16[1,256,4096]{2,1,0:T(8,128)(2,1)S(1)} %bitcast.4) | data formatting | bytes 4194304
